TPU v7x, 32 devices: a whole 2x2x4 slice. The times are simulated.
32 devices in a mesh: band: 8 (over z, core), grid: 4 (over y, x).
Axes of the slice: x: 2, y: 2, z: 4, core: 2. Of those that a mesh axis runs over, the one named last changes fastest.
Arguments:
- orbitals: float32 [8, 48, 2304], P('band', 'grid'), may hold values from -6 to 6
Outputs:
- compressed: float32 [8, 48, 2304], P('band', 'grid')
All inputs are finite; a program needn't handle non-finite values.
Results may differ from a plain program's by a relative error of at most 0.000092.
Values sent between devices are 32-bit elements; how exact they have to be, the bound alone decides.
A program may use at most 64 MiB of HBM per device.

v0:
```python
import functools
import math

import jax
import jax.numpy as jnp
import numpy as np
from jax import lax
from jax.experimental import pallas as pl
from jax.experimental.pallas import tpu as pltpu
from jax.sharding import PartitionSpec as P

MESH = pl.DeviceIdType.MESH
F32 = jnp.float32
BF16 = jnp.bfloat16
coulomb_scale = 50.0


def real_basis(length):
    n = np.arange(length)[:, None]
    m = np.arange(length)[None, :]
    angle = 2.0 * math.pi * ((n * np.minimum(m, length - m)) % length) / length
    table = np.where(m <= length // 2, np.cos(angle), np.sin(angle))
    weight = np.where((m == 0) | (2 * m == length), 1.0, 2.0)
    return table * np.sqrt(weight / length)


def split(value):
    high = value.astype(BF16)
    return high, (value - high.astype(F32)).astype(BF16)


def times(value, high, low, contract=((1,), (0,))):
    dims = (contract, ((), ()))
    value_high, value_low = split(value)
    dot = functools.partial(lax.dot_general, dimension_numbers=dims, preferred_element_type=F32)
    return dot(value_high, high) + (dot(value_low, high) + dot(value_high, low))


def times_left(high, low, value):
    dims = (((1,), (1,)), ((), ()))
    value_high, value_low = split(value)
    dot = functools.partial(lax.dot_general, dimension_numbers=dims, preferred_element_type=F32)
    return dot(high, value_high) + (dot(high, value_low) + dot(low, value_high))


def flat(value):
    return value.reshape(value.shape[0] * value.shape[1], value.shape[2])


def kernel(
    bands, grids, length,
    phi, tables, out,
    slabs, own, part, field, sums, exs, proj_grid, proj_band,
    dense_own, dense_part, work, coulomb, dense_field, column,
    sem_local, slab_send, slab_recv, fwd_send,
    own_send, own_recv, part_send, part_recv, pfwd_send, pfwd_recv,
    sum_send, sum_recv, ex_send, ex_recv, xfwd_send,
    pg_send, pg_recv, pb_send, pb_recv,
):
    b = lax.axis_index("band")
    g = lax.axis_index("grid")
    p = b // 2
    c = b % 2
    sibling = p * 2 + (1 - c)
    rows = length // grids
    pairs = bands // 2
    step = 8
    chunk = step * length

    def remote(src, dst, send, recv, band, grid):
        return pltpu.make_async_remote_copy(
            src_ref=src, dst_ref=dst, send_sem=send, recv_sem=recv,
            device_id=(band, grid), device_id_type=MESH,
        )

    local = pltpu.make_async_copy(phi, slabs.at[b], sem_local)
    local.start()

    barrier = pltpu.get_barrier_semaphore()
    for off in range(1, bands):
        pl.semaphore_signal(barrier, inc=1, device_id=(lax.rem(b + off, bands), g), device_id_type=MESH)
    for off in range(1, grids):
        pl.semaphore_signal(barrier, inc=1, device_id=(b, lax.rem(g + off, grids)), device_id_type=MESH)
    pl.semaphore_wait(barrier, bands + grids - 2)

    waits = []

    def go(copy):
        copy.start()
        waits.append(copy)

    for off in range(1, pairs):
        peer = lax.rem(p + off, pairs) * 2 + c
        go(remote(phi, slabs.at[b], slab_send.at[off], slab_recv.at[b], peer, g))
    for off in range(1, grids):
        go(remote(phi, own.at[g], own_send.at[off], own_recv.at[g], b, lax.rem(g + off, grids)))
    go(remote(phi, slabs.at[b], slab_send.at[0], slab_recv.at[b], sibling, g))

    def freq(shape, dim, base):
        m = lax.broadcasted_iota(jnp.int32, shape, dim) + base
        f = jnp.minimum(m, length - m).astype(F32)
        return f * f

    def coulomb_step(i, carry):
        shape = (step, length, length)
        squared = freq(shape, 0, i * step) + freq(shape, 1, 0) + freq(shape, 2, 0)
        coulomb[pl.ds(i * step, step)] = jnp.where(
            squared > 0.0, coulomb_scale / jnp.maximum(squared, 1.0), 0.0
        )
        return carry

    lax.fori_loop(0, length // step, coulomb_step, 0)
    local.wait()

    def to_partner(pair):
        copy = remote(
            slabs.at[pair * 2 + c], part.at[c, g], part_send.at[pair], part_recv.at[g], b, pair
        )

        @pl.when(pair != g)
        def _():
            copy.start()

    to_partner(p)
    for off in range(1, pairs):
        pair = lax.rem(p + off, pairs)
        band = pair * 2 + c
        remote(phi, slabs.at[band], slab_send.at[0], slab_recv.at[band], sibling, g).wait_recv()
        to_partner(pair)
        go(remote(slabs.at[band], slabs.at[band], fwd_send.at[off], slab_recv.at[band], sibling, g))

    for off in range(1, grids):
        other = lax.rem(g + off, grids)
        remote(phi, part.at[c, other], part_send.at[0], part_recv.at[other], b, other).wait_recv()
        go(remote(part.at[c, other], part.at[c, other], pfwd_send.at[off], pfwd_recv.at[other], sibling, g))

    for off in range(1, grids):
        other = lax.rem(g + off, grids)
        remote(phi, own.at[other], own_send.at[0], own_recv.at[other], b, other).wait_recv()
    own[g] = phi[...]
    for off in range(pairs):
        band = lax.rem(p + off, pairs) * 2 + (1 - c)
        remote(phi, slabs.at[band], slab_send.at[0], slab_recv.at[band], sibling, g).wait_recv()
    for k in range(2):
        part[k, g] = slabs[2 * g + k]
    for off in range(1, grids):
        other = lax.rem(g + off, grids)
        remote(phi, part.at[1 - c, other], part_send.at[0], pfwd_recv.at[other], sibling, g).wait_recv()

    for s in range(grids):
        dense_own[s * rows:(s + 1) * rows, :] = own[s]
        for k in range(2):
            dense_part[k, s * rows:(s + 1) * rows, :] = part[k, s]

    q_high, q_low, t_high, t_low = (tables[n] for n in range(4))

    def swap(value):
        return jnp.swapaxes(value, 1, 2)

    def unflat(value):
        return value.reshape(value.shape[0] // length, length, length)

    def one_pair(k, carry):
        def stage_in(i, carry):
            lanes = pl.ds(pl.multiple_of(i * chunk, 128), chunk)
            density = dense_own[:, lanes] * dense_part[k, :, lanes]
            first = unflat(times(density.T, q_high, q_low))
            second = unflat(times(flat(swap(first)), q_high, q_low))
            work[pl.ds(i * step, step)] = second
            return carry

        def stage_mid(i, carry):
            here = pl.ds(pl.multiple_of(i * step, step), step)
            value = jnp.swapaxes(work[:, here, :], 0, 1)
            value = unflat(times(flat(swap(value)), q_high, q_low))
            value = value * coulomb[pl.ds(i * step, step)]
            value = unflat(times(flat(value), t_high, t_low))
            work[:, here, :] = jnp.swapaxes(swap(value), 0, 1)
            return carry

        def stage_out(i, carry):
            lanes = pl.ds(pl.multiple_of(i * chunk, 128), chunk)
            value = unflat(times(flat(work[pl.ds(i * step, step)]), t_high, t_low))
            potential = times_left(q_high, q_low, flat(swap(value)))
            term = dense_part[k, :, lanes] * potential

            @pl.when(k == 0)
            def _():
                dense_field[:, lanes] = term

            @pl.when(k != 0)
            def _():
                dense_field[:, lanes] += term

            return carry

        lax.fori_loop(0, length // step, stage_in, 0)
        lax.fori_loop(0, length // step, stage_mid, 0)
        lax.fori_loop(0, length // step, stage_out, 0)
        return carry

    lax.fori_loop(0, 2, one_pair, 0)

    for s in range(grids):
        field[s] = dense_field[s * rows:(s + 1) * rows, :]
    for off in range(1, grids):
        other = lax.rem(g + off, grids)
        go(remote(field.at[other], sums.at[g], sum_send.at[off], sum_recv.at[g], b, other))
    exchange = field[g]
    for off in range(1, grids):
        other = lax.rem(g + off, grids)
        remote(phi, sums.at[other], sum_send.at[0], sum_recv.at[other], b, other).wait_recv()
        exchange = exchange + sums[other]
    exs[b] = -exchange
    for off in range(1, pairs):
        peer = lax.rem(p + off, pairs) * 2 + c
        go(remote(exs.at[b], exs.at[b], ex_send.at[off], ex_recv.at[b], peer, g))
    go(remote(exs.at[b], exs.at[b], ex_send.at[0], ex_recv.at[b], sibling, g))

    lane = lax.broadcasted_iota(jnp.int32, (8, 128), 1)
    mine = exs[b]
    total = jnp.zeros((8, 128), F32)
    for k in range(bands):
        product = jnp.sum(slabs[k] * mine, axis=0, keepdims=True)
        product = jnp.sum(product, axis=1, keepdims=True)
        total = jnp.where(lane == k, product, total)
    proj_grid[g] = total
    for off in range(1, grids):
        other = lax.rem(g + off, grids)
        go(remote(proj_grid.at[g], proj_grid.at[g], pg_send.at[off], pg_recv.at[g], b, other))
    for off in range(1, grids):
        other = lax.rem(g + off, grids)
        remote(column, proj_grid.at[other], pg_send.at[0], pg_recv.at[other], b, other).wait_recv()
    total = proj_grid[0]
    for s in range(1, grids):
        total = total + proj_grid[s]
    proj_band[b] = total
    for off in range(1, bands):
        other = lax.rem(b + off, bands)
        go(remote(proj_band.at[b], proj_band.at[b], pb_send.at[off], pb_recv.at[b], other, g))

    for off in range(1, pairs):
        band = lax.rem(p + off, pairs) * 2 + c
        remote(phi, exs.at[band], ex_send.at[0], ex_recv.at[band], sibling, g).wait_recv()
        go(remote(exs.at[band], exs.at[band], xfwd_send.at[off], ex_recv.at[band], sibling, g))

    for off in range(1, bands):
        other = lax.rem(b + off, bands)
        remote(column, proj_band.at[other], pb_send.at[0], pb_recv.at[other], other, g).wait_recv()

    row = lax.broadcasted_iota(jnp.int32, (bands, 128), 0)
    col = lax.broadcasted_iota(jnp.int32, (bands, 128), 1)
    matrix = jnp.concatenate([proj_band[l][0:1, :] for l in range(bands)], axis=0)
    mirrored = jnp.zeros((bands, 128), F32)
    for l in range(bands):
        entry = jnp.sum(jnp.where(col == l, matrix, 0.0), axis=1, keepdims=True)
        flipped = jnp.sum(jnp.where(row == col, entry, 0.0), axis=0, keepdims=True)
        mirrored = jnp.where(row == l, flipped, mirrored)
    definite = (matrix + mirrored) * (-0.5 / float(length**3))
    definite = jnp.where(col < bands, definite, jnp.where(col == row + bands, 1.0, 0.0))
    for j in range(bands):
        line = jnp.sum(jnp.where(row == j, definite, 0.0), axis=0, keepdims=True)
        entry = jnp.sum(jnp.where(col == j, definite, 0.0), axis=1, keepdims=True)
        pivot = jnp.sum(jnp.where(col[0:1] == j, line, 0.0), axis=1, keepdims=True)
        definite = definite - jnp.where(row > j, (entry / pivot) * line, 0.0)
    pick = jnp.sum(jnp.where(row == b, definite, 0.0), axis=0, keepdims=True)
    pivot = jnp.sum(jnp.where(col[0:1] == b, pick, 0.0), axis=1, keepdims=True)
    pick = pick / jnp.sqrt(pivot)

    for off in range(pairs):
        band = lax.rem(p + off, pairs) * 2 + (1 - c)
        remote(phi, exs.at[band], ex_send.at[0], ex_recv.at[band], sibling, g).wait_recv()
    result = jnp.zeros_like(mine)
    for l in range(bands):
        weight = jnp.sum(jnp.where(col[0:1] == bands + l, pick, 0.0), axis=1, keepdims=True)
        result = result + weight * exs[l]
    out[...] = result

    for copy in waits:
        copy.wait_send()
    for off in range(pairs):
        pair = lax.rem(p + off, pairs)
        copy = remote(slabs.at[pair * 2 + c], part.at[c, g], part_send.at[pair], part_recv.at[g], b, pair)

        @pl.when(pair != g)
        def _(copy=copy):
            copy.wait_send()


def per_device(bands, grids, orbitals):
    blocks, rows, cells = orbitals.shape
    length = rows * grids
    assert blocks == 1 and bands == 2 * grids and length * length == cells
    basis = real_basis(length)
    parts = []
    for table in (basis, basis.T):
        high = table.astype(np.float32).astype(BF16)
        parts += [high, (table - high.astype(np.float64)).astype(np.float32).astype(BF16)]
    tables = jnp.asarray(np.stack(parts))
    slab = (rows, cells)
    dma = lambda n: pltpu.SemaphoreType.DMA((n,))
    vmem = lambda *shape: pltpu.VMEM(shape, F32)
    pairs = bands // 2
    result = pl.pallas_call(
        functools.partial(kernel, bands, grids, length),
        out_shape=jax.ShapeDtypeStruct(slab, F32),
        in_specs=[pl.BlockSpec(memory_space=pltpu.VMEM)] * 2,
        out_specs=pl.BlockSpec(memory_space=pltpu.VMEM),
        scratch_shapes=[
            vmem(bands, *slab), vmem(grids, *slab), vmem(2, grids, *slab),
            vmem(grids, *slab), vmem(grids, *slab), vmem(bands, *slab),
            vmem(grids, 8, 128), vmem(bands, 8, 128),
            vmem(length, cells), vmem(2, length, cells),
            vmem(length, length, length), vmem(length, length, length),
            vmem(length, cells), vmem(8, 128),
            pltpu.SemaphoreType.DMA, dma(pairs), dma(bands), dma(pairs),
            dma(grids), dma(grids), dma(pairs), dma(grids), dma(grids), dma(grids),
            dma(grids), dma(grids), dma(pairs), dma(bands), dma(pairs),
            dma(grids), dma(grids), dma(bands), dma(bands),
        ],
        compiler_params=pltpu.CompilerParams(
            collective_id=0, has_side_effects=True, vmem_limit_bytes=40 * 1024 * 1024
        ),
    )(orbitals.reshape(slab), tables)
    return result.reshape(orbitals.shape)


def solution(mesh):
    bands, grids = mesh.shape["band"], mesh.shape["grid"]
    return jax.shard_map(
        functools.partial(per_device, bands, grids), mesh=mesh,
        in_specs=(P("band", "grid", None),), out_specs=P("band", "grid", None), check_vma=False,
    )
```

profile of v0, /device:TPU:0, one launch (start us, length us, event | category | flops | bytes accessed | tf_op | source)
XLA Modules:
  0.0 78.1 jit_solution(611173110284584678)
XLA Ops:
  0.0 0.0 copy-start
  0.0 0.9 %copy.6 = f32[1,12,2304]{2,1,0:T(8,128)S(1)} copy(f32[1,12,2304]{2,0,1:T(1,128)} %param.2) | data formatting | bytes 221184
  0.9 0.0 copy-done
  0.9 76.4 %shard_map.28 = f32[12,2304]{1,0:T(8,128)S(1)} custom-call(f32[12,2304]{1,0:T(8,128)S(1)} %bitcast.5, bf16[4,48,48]{2,1,0:T(8,128)(2,1)S(1)} %copy-done), custom_call_target="tpu_custom_call" | custom-call | tf_op jit(solution)/shard_map/pallas_call | solution.py:304
  77.4 0.8 copy.3
Async XLA Ops:
  0.0 0.9 %copy-start = (bf16[4,48,48]{2,1,0:T(8,128)(2,1)S(1)}, bf16[4,48,48]{2,1,0:T(8,128)(2,1)}, u32[]{:S(2)}) copy-start(bf16[4,48,48]{2,1,0:T(8,128)(2,1)} %constant.2.clone.tables) | copy-start | bytes 55300
where the time goes:
time: 78.3 us; the launch traced here: 78.1 us
  Pallas kernels  76.4 us (98%)
  local copies, waits for them, and re-layouts  1.68 us (2%)
    pallas_call x1, Pallas kernels, per_device(): pl.pallas_call(functools.partial(kernel, bands, grids, length), out_shape...  76.4 us

commit v1 on v0

v1 whole, which is shorter than its diff:
```python
import functools
import math

import jax
import jax.numpy as jnp
import numpy as np
from jax import lax
from jax.experimental import pallas as pl
from jax.experimental.pallas import tpu as pltpu
from jax.sharding import PartitionSpec as P

MESH = pl.DeviceIdType.MESH
F32 = jnp.float32
BF16 = jnp.bfloat16
coulomb_scale = 50.0


def real_basis(length):
    n = np.arange(length)[:, None]
    m = np.arange(length)[None, :]
    angle = 2.0 * math.pi * ((n * np.minimum(m, length - m)) % length) / length
    table = np.where(m <= length // 2, np.cos(angle), np.sin(angle))
    weight = np.where((m == 0) | (2 * m == length), 1.0, 2.0)
    return table * np.sqrt(weight / length)


def split(value):
    high = value.astype(BF16)
    return high, (value - high.astype(F32)).astype(BF16)


def times(value, high, low, contract=((1,), (0,))):
    dims = (contract, ((), ()))
    value_high, value_low = split(value)
    dot = functools.partial(lax.dot_general, dimension_numbers=dims, preferred_element_type=F32)
    return dot(value_high, high) + (dot(value_low, high) + dot(value_high, low))


def times_left(high, low, value):
    dims = (((1,), (1,)), ((), ()))
    value_high, value_low = split(value)
    dot = functools.partial(lax.dot_general, dimension_numbers=dims, preferred_element_type=F32)
    return dot(high, value_high) + (dot(high, value_low) + dot(low, value_high))


def flat(value):
    return value.reshape(value.shape[0] * value.shape[1], value.shape[2])


def kernel(
    bands, grids, length, pieces,
    phi, tables, out,
    slabs, own, part, field, sums, exs, proj_grid, proj_band,
    dense_own, dense_part, work, coulomb, dense_field,
    sem_local, slab_send, slab_recv, fwd_send,
    own_send, own_recv, part_send, part_recv, pfwd_send, pfwd_recv,
    sum_send, sum_recv, ex_send, ex_recv, xfwd_send,
    pg_send, pg_recv, pb_send, pb_recv,
):
    b = lax.axis_index("band")
    g = lax.axis_index("grid")
    p = b // 2
    c = b % 2
    sibling = p * 2 + (1 - c)
    rows = length // grids
    pairs = bands // 2
    step = 8
    chunk = step * length
    chunks = length // step
    width = length * length // pieces
    per_piece = chunks // pieces

    def remote(src, dst, send, recv, band, grid):
        return pltpu.make_async_remote_copy(
            src_ref=src, dst_ref=dst, send_sem=send, recv_sem=recv,
            device_id=(band, grid), device_id_type=MESH,
        )

    def cut(q):
        return pl.ds(q * width, width)

    local = pltpu.make_async_copy(phi, slabs.at[b], sem_local)
    local.start()

    barrier = pltpu.get_barrier_semaphore()
    for off in range(1, bands):
        pl.semaphore_signal(barrier, inc=1, device_id=(lax.rem(b + off, bands), g), device_id_type=MESH)
    for off in range(1, grids):
        pl.semaphore_signal(barrier, inc=1, device_id=(b, lax.rem(g + off, grids)), device_id_type=MESH)

    def freq(shape, dim, base):
        m = lax.broadcasted_iota(jnp.int32, shape, dim) + base
        f = jnp.minimum(m, length - m).astype(F32)
        return f * f

    def coulomb_step(i, carry):
        shape = (step, length, length)
        squared = freq(shape, 0, i * step) + freq(shape, 1, 0) + freq(shape, 2, 0)
        coulomb[pl.ds(i * step, step)] = jnp.where(
            squared > 0.0, coulomb_scale / jnp.maximum(squared, 1.0), 0.0
        )
        return carry

    lax.fori_loop(0, chunks, coulomb_step, 0)
    local.wait()
    pl.semaphore_wait(barrier, bands + grids - 2)

    waits = []

    def go(copy):
        copy.start()
        waits.append(copy)

    for q in range(pieces):
        for off in range(1, pairs):
            peer = lax.rem(p + off, pairs) * 2 + c
            go(remote(phi.at[:, cut(q)], slabs.at[b, :, cut(q)],
                      slab_send.at[off, q], slab_recv.at[b, q], peer, g))
        for off in range(1, grids):
            go(remote(phi.at[:, cut(q)], own.at[g, :, cut(q)],
                      own_send.at[off, q], own_recv.at[g, q], b, lax.rem(g + off, grids)))
        go(remote(phi.at[:, cut(q)], slabs.at[b, :, cut(q)],
                  slab_send.at[0, q], slab_recv.at[b, q], sibling, g))

    def partner_copy(pair, q):
        return remote(
            slabs.at[pair * 2 + c, :, cut(q)], part.at[c, g, :, cut(q)],
            part_send.at[pair, q], part_recv.at[g, q], b, pair,
        )

    def to_partner(pair, q):
        @pl.when(pair != g)
        def _():
            partner_copy(pair, q).start()

    def slab_arrival(band, q):
        here = slabs.at[band, :, cut(q)]
        remote(here, here, slab_send.at[0, q], slab_recv.at[band, q], sibling, g).wait_recv()

    def pass_slabs(q):
        to_partner(p, q)
        for off in range(1, pairs):
            pair = lax.rem(p + off, pairs)
            band = pair * 2 + c
            slab_arrival(band, q)
            to_partner(pair, q)
            here = slabs.at[band, :, cut(q)]
            go(remote(here, here, fwd_send.at[off, q], slab_recv.at[band, q], sibling, g))

    def pass_partners(q):
        for off in range(1, grids):
            other = lax.rem(g + off, grids)
            here = part.at[c, other, :, cut(q)]
            remote(here, here, part_send.at[0, q], part_recv.at[other, q], b, other).wait_recv()
            go(remote(here, here, pfwd_send.at[off, q], pfwd_recv.at[other, q], sibling, g))

    def collect(q):
        slab_arrival(2 * g + 1 - c, q)
        for off in range(1, grids):
            other = lax.rem(g + off, grids)
            here = own.at[other, :, cut(q)]
            remote(here, here, own_send.at[0, q], own_recv.at[other, q], b, other).wait_recv()
            here = part.at[1 - c, other, :, cut(q)]
            remote(here, here, part_send.at[0, q], pfwd_recv.at[other, q], sibling, g).wait_recv()
        own[g, :, cut(q)] = phi[:, cut(q)]
        for k in range(2):
            part[k, g, :, cut(q)] = slabs[2 * g + k, :, cut(q)]
        for s in range(grids):
            here = slice(s * rows, (s + 1) * rows)
            dense_own[here, cut(q)] = own[s, :, cut(q)]
            for k in range(2):
                dense_part[k, here, cut(q)] = part[k, s, :, cut(q)]

    q_high, q_low, t_high, t_low = (tables[n] for n in range(4))

    def swap(value):
        return jnp.swapaxes(value, 1, 2)

    def unflat(value):
        return value.reshape(value.shape[0] // length, length, length)

    def lanes_of(i):
        return pl.ds(pl.multiple_of(i * chunk, 128), chunk)

    def stage_in(i, carry):
        lanes = lanes_of(i)
        for k in range(2):
            density = dense_own[:, lanes] * dense_part[k, :, lanes]
            first = unflat(times(density.T, q_high, q_low))
            work[k, pl.ds(i * step, step)] = unflat(times(flat(swap(first)), q_high, q_low))
        return carry

    def stage_mid(i, carry):
        here = pl.ds(pl.multiple_of(i * step, step), step)
        for k in range(2):
            value = jnp.swapaxes(work[k, :, here, :], 0, 1)
            value = unflat(times(flat(swap(value)), q_high, q_low))
            value = value * coulomb[pl.ds(i * step, step)]
            value = unflat(times(flat(value), t_high, t_low))
            work[k, :, here, :] = jnp.swapaxes(swap(value), 0, 1)
        return carry

    def send_sums(i):
        lanes = lanes_of(i)
        for off in range(1, grids):
            other = lax.rem(g + off, grids)
            remote(field.at[other, :, lanes], sums.at[g, :, lanes],
                   sum_send.at[off, i], sum_recv.at[g, i], b, other).start()

    def stage_out(i, carry):
        lanes = lanes_of(i)
        term = None
        for k in range(2):
            value = unflat(times(flat(work[k, pl.ds(i * step, step)]), t_high, t_low))
            here = dense_part[k, :, lanes] * times_left(q_high, q_low, flat(swap(value)))
            term = here if term is None else term + here
        dense_field[...] = term
        for s in range(grids):
            field[s, :, lanes] = dense_field[s * rows:(s + 1) * rows, :]

        @pl.when(i > 0)
        def _():
            send_sums(i - 1)

        return carry

    columns = [None] * bands

    def exchange_piece(q):
        for i in range(q * per_piece, (q + 1) * per_piece):
            lanes = pl.ds(i * chunk, chunk)
            for off in range(1, grids):
                other = lax.rem(g + off, grids)
                here = sums.at[other, :, lanes]
                remote(here, here, sum_send.at[0, i], sum_recv.at[other, i], b, other).wait_recv()
        value = field[g, :, cut(q)]
        for off in range(1, grids):
            value = value + sums[lax.rem(g + off, grids), :, cut(q)]
        value = -value
        exs[b, :, cut(q)] = value
        for k in range(bands):
            product = jnp.sum(slabs[k, :, cut(q)] * value, axis=0, keepdims=True)
            product = sum(product[:, n:n + 128] for n in range(0, width, 128))
            columns[k] = product if columns[k] is None else columns[k] + product
        here = exs.at[b, :, cut(q)]
        for off in range(1, pairs):
            peer = lax.rem(p + off, pairs) * 2 + c
            go(remote(here, here, ex_send.at[off, q], ex_recv.at[b, q], peer, g))
        go(remote(here, here, ex_send.at[0, q], ex_recv.at[b, q], sibling, g))

    for q in range(pieces):
        pass_slabs(q)
        if q >= 1:
            pass_partners(q - 1)
    for q in range(pieces):
        collect(q)
        lax.fori_loop(q * per_piece, (q + 1) * per_piece, stage_in, 0)
        if q == 0:
            pass_partners(pieces - 1)
    lax.fori_loop(0, chunks, stage_mid, 0)
    for q in range(pieces):
        for off in range(pairs):
            pair = lax.rem(p + off, pairs)

            @pl.when(pair != g)
            def _(pair=pair, q=q):
                slab_arrival(pair * 2 + 1 - c, q)

    for q in range(pieces):
        lax.fori_loop(q * per_piece, (q + 1) * per_piece, stage_out, 0)
        if q >= 1:
            exchange_piece(q - 1)
    send_sums(chunks - 1)
    exchange_piece(pieces - 1)

    total = jnp.sum(jnp.concatenate(columns, axis=0), axis=1, keepdims=True)
    proj_grid[g] = jnp.broadcast_to(total, (bands, 128))
    for off in range(1, grids):
        other = lax.rem(g + off, grids)
        go(remote(proj_grid.at[g], proj_grid.at[g], pg_send.at[off], pg_recv.at[g], b, other))

    def ex_arrival(band, q):
        here = exs.at[band, :, cut(q)]
        remote(here, here, ex_send.at[0, q], ex_recv.at[band, q], sibling, g).wait_recv()

    def pass_exchange(q):
        for off in range(1, pairs):
            band = lax.rem(p + off, pairs) * 2 + c
            ex_arrival(band, q)
            here = exs.at[band, :, cut(q)]
            go(remote(here, here, xfwd_send.at[off, q], ex_recv.at[band, q], sibling, g))

    pass_exchange(0)
    for off in range(1, grids):
        other = lax.rem(g + off, grids)
        here = proj_grid.at[other]
        remote(here, here, pg_send.at[0], pg_recv.at[other], b, other).wait_recv()
    total = proj_grid[0]
    for s in range(1, grids):
        total = total + proj_grid[s]
    proj_band[b] = total
    for off in range(1, bands):
        other = lax.rem(b + off, bands)
        go(remote(proj_band.at[b], proj_band.at[b], pb_send.at[off], pb_recv.at[b], other, g))
    for q in range(1, pieces):
        pass_exchange(q)
    for off in range(1, bands):
        other = lax.rem(b + off, bands)
        here = proj_band.at[other]
        remote(here, here, pb_send.at[0], pb_recv.at[other], other, g).wait_recv()

    row = lax.broadcasted_iota(jnp.int32, (bands, 128), 0)
    col = lax.broadcasted_iota(jnp.int32, (bands, 128), 1)
    matrix = jnp.zeros((bands, 128), F32)
    mirrored = jnp.zeros((bands, 128), F32)
    for l in range(bands):
        entries = proj_band[l]
        matrix = jnp.where(col == l, entries, matrix)
        flipped = jnp.sum(jnp.where(row == col, entries, 0.0), axis=0, keepdims=True)
        mirrored = jnp.where(row == l, flipped, mirrored)
    definite = (matrix + mirrored) * (-0.5 / float(length**3))
    definite = jnp.where(col < bands, definite, jnp.where(col == row + bands, 1.0, 0.0))
    for j in range(bands - 1):
        line = definite[j:j + 1, :]
        ratio = definite[:, j:j + 1] / definite[j:j + 1, j:j + 1]
        definite = definite - jnp.where(row > j, ratio * line, 0.0)
    pick = jnp.sum(jnp.where(row == b, definite, 0.0), axis=0, keepdims=True)
    pivot = jnp.sum(jnp.where(col[0:1] == b, pick, 0.0), axis=1, keepdims=True)
    pick = pick / jnp.sqrt(pivot)

    for q in range(pieces):
        for off in range(pairs):
            ex_arrival(lax.rem(p + off, pairs) * 2 + (1 - c), q)
    result = jnp.zeros(phi.shape, F32)
    for l in range(bands):
        result = result + pick[:, bands + l:bands + l + 1] * exs[l]
    out[...] = result

    for copy in waits:
        copy.wait_send()
    for i in range(chunks):
        lanes = pl.ds(i * chunk, chunk)
        for off in range(1, grids):
            other = lax.rem(g + off, grids)
            remote(field.at[other, :, lanes], sums.at[g, :, lanes],
                   sum_send.at[off, i], sum_recv.at[g, i], b, other).wait_send()
    for q in range(pieces):
        for off in range(pairs):
            pair = lax.rem(p + off, pairs)

            @pl.when(pair != g)
            def _(pair=pair, q=q):
                partner_copy(pair, q).wait_send()


def per_device(bands, grids, orbitals):
    blocks, rows, cells = orbitals.shape
    length = rows * grids
    assert blocks == 1 and bands == 2 * grids and length * length == cells
    basis = real_basis(length)
    parts = []
    for table in (basis, basis.T):
        high = table.astype(np.float32).astype(BF16)
        parts += [high, (table - high.astype(np.float64)).astype(np.float32).astype(BF16)]
    tables = jnp.asarray(np.stack(parts))
    slab = (rows, cells)
    dma = lambda *n: pltpu.SemaphoreType.DMA(n)
    vmem = lambda *shape: pltpu.VMEM(shape, F32)
    pairs = bands // 2
    pieces = 3
    chunks = length // 8
    result = pl.pallas_call(
        functools.partial(kernel, bands, grids, length, pieces),
        out_shape=jax.ShapeDtypeStruct(slab, F32),
        in_specs=[pl.BlockSpec(memory_space=pltpu.VMEM)] * 2,
        out_specs=pl.BlockSpec(memory_space=pltpu.VMEM),
        scratch_shapes=[
            vmem(bands, *slab), vmem(grids, *slab), vmem(2, grids, *slab),
            vmem(grids, *slab), vmem(grids, *slab), vmem(bands, *slab),
            vmem(grids, bands, 128), vmem(bands, bands, 128),
            vmem(length, cells), vmem(2, length, cells),
            vmem(2, length, length, length), vmem(length, length, length),
            vmem(length, 8 * length),
            pltpu.SemaphoreType.DMA,
            dma(pairs, pieces), dma(bands, pieces), dma(pairs, pieces),
            dma(grids, pieces), dma(grids, pieces), dma(pairs, pieces), dma(grids, pieces),
            dma(grids, pieces), dma(grids, pieces),
            dma(grids, chunks), dma(grids, chunks),
            dma(pairs, pieces), dma(bands, pieces), dma(pairs, pieces),
            dma(grids), dma(grids), dma(bands), dma(bands),
        ],
        compiler_params=pltpu.CompilerParams(
            collective_id=0, has_side_effects=True, vmem_limit_bytes=40 * 1024 * 1024
        ),
    )(orbitals.reshape(slab), tables)
    return result.reshape(orbitals.shape)


def solution(mesh):
    bands, grids = mesh.shape["band"], mesh.shape["grid"]
    return jax.shard_map(
        functools.partial(per_device, bands, grids), mesh=mesh,
        in_specs=(P("band", "grid", None),), out_specs=P("band", "grid", None), check_vma=False,
    )
```

time: 78.3 us -> 60.7 us (0.78)
  Pallas kernels: 76.4 us -> 58.9 us
    pallas_call x1, Pallas kernels: 76.4 us -> 58.9 us  [per_device(): pl.pallas_call(functools.partial(kernel, bands, grids, length, pieces), o...]
where the time goes in v1:
time: 60.7 us; the launch traced here: 60.6 us
  Pallas kernels  58.9 us (97%)
  local copies, waits for them, and re-layouts  1.68 us (3%)
    pallas_call x1, Pallas kernels, per_device(): pl.pallas_call(functools.partial(kernel, bands, grids, length, pieces), o...  58.9 us

profile of v1, /device:TPU:0, one launch (start us, length us, event | category | flops | bytes accessed | tf_op | source)
XLA Modules:
  0.0 60.6 jit_solution(2510355280868486777)
XLA Ops:
  0.0 0.0 copy-start
  0.0 0.9 %copy.6 = f32[1,12,2304]{2,1,0:T(8,128)S(1)} copy(f32[1,12,2304]{2,0,1:T(1,128)} %param.2) | data formatting | bytes 221184
  0.9 0.0 copy-done
  0.9 58.9 %shard_map.28 = f32[12,2304]{1,0:T(8,128)S(1)} custom-call(f32[12,2304]{1,0:T(8,128)S(1)} %bitcast.5, bf16[4,48,48]{2,1,0:T(8,128)(2,1)S(1)} %copy-done), custom_call_target="tpu_custom_call" | custom-call | tf_op jit(solution)/shard_map/pallas_call | solution.py:372
  59.8 0.8 %copy.3 = f32[1,12,2304]{2,0,1:T(1,128)} copy(f32[1,12,2304]{2,1,0:T(8,128)S(1)} %bitcast.4) | data formatting | bytes 221184 | tf_op jit(solution)/shard_map/reshape | solution.py:396
Async XLA Ops:
  0.0 0.9 %copy-start = (bf16[4,48,48]{2,1,0:T(8,128)(2,1)S(1)}, bf16[4,48,48]{2,1,0:T(8,128)(2,1)}, u32[]{:S(2)}) copy-start(bf16[4,48,48]{2,1,0:T(8,128)(2,1)} %constant.2.clone.tables) | copy-start | bytes 55300

commit v2 on v1

--- a/solution.py
+++ b/solution.py
@@ -268,10 +268,9 @@
 
     for q in range(pieces):
         lax.fori_loop(q * per_piece, (q + 1) * per_piece, stage_out, 0)
-        if q >= 1:
-            exchange_piece(q - 1)
     send_sums(chunks - 1)
-    exchange_piece(pieces - 1)
+    for q in range(pieces):
+        exchange_piece(q)
 
     total = jnp.sum(jnp.concatenate(columns, axis=0), axis=1, keepdims=True)
     proj_grid[g] = jnp.broadcast_to(total, (bands, 128))

time: 60.7 us -> 58.7 us (0.967)
  Pallas kernels: 58.9 us -> 56.9 us
    pallas_call x1, Pallas kernels: 58.9 us -> 56.9 us  [per_device(): pl.pallas_call(functools.partial(kernel, bands, grids, length, pieces), o...]
where the time goes in v2:
time: 58.7 us; the launch traced here: 58.6 us
  Pallas kernels  56.9 us (97%)
  local copies, waits for them, and re-layouts  1.68 us (3%)
    pallas_call x1, Pallas kernels, per_device(): pl.pallas_call(functools.partial(kernel, bands, grids, length, pieces), o...  56.9 us

profile of v2, /device:TPU:0, one launch (start us, length us, event | category | flops | bytes accessed | tf_op | source)
XLA Modules:
  0.0 58.6 jit_solution(4890593687500078259)
XLA Ops:
  0.0 0.0 copy-start
  0.0 0.9 %copy.6 = f32[1,12,2304]{2,1,0:T(8,128)S(1)} copy(f32[1,12,2304]{2,0,1:T(1,128)} %param.2) | data formatting | bytes 221184
  0.9 0.0 copy-done
  0.9 56.9 %shard_map.28 = f32[12,2304]{1,0:T(8,128)S(1)} custom-call(f32[12,2304]{1,0:T(8,128)S(1)} %bitcast.5, bf16[4,48,48]{2,1,0:T(8,128)(2,1)S(1)} %copy-done), custom_call_target="tpu_custom_call" | custom-call | tf_op jit(solution)/shard_map/pallas_call | solution.py:371
  57.8 0.8 %copy.3 = f32[1,12,2304]{2,0,1:T(1,128)} copy(f32[1,12,2304]{2,1,0:T(8,128)S(1)} %bitcast.4) | data formatting | bytes 221184 | tf_op jit(solution)/shard_map/reshape | solution.py:395
Async XLA Ops:
  0.0 0.9 %copy-start = (bf16[4,48,48]{2,1,0:T(8,128)(2,1)S(1)}, bf16[4,48,48]{2,1,0:T(8,128)(2,1)}, u32[]{:S(2)}) copy-start(bf16[4,48,48]{2,1,0:T(8,128)(2,1)} %constant.2.clone.tables) | copy-start | bytes 55300
